TPU v7x, 8 devices: a whole 2x2x1 slice. The times are simulated.
8 devices in a mesh: batch: 1 (over z), dap: 8 (over y, x, core).
Axes of the slice: x: 2, y: 2, z: 1, core: 2. Of those that a mesh axis runs over, the one named last changes fastest.
Arguments:
- z_pair: bfloat16 [256, 256, 128], P(('batch', 'dap'))
- msa_feat: bfloat16 [512, 256, 64], P(None, ('batch', 'dap'))
- ln_scale: bfloat16 [64], replicated
- ln_offset: bfloat16 [64], replicated
- w_a: bfloat16 [64, 32], replicated
- b_a: bfloat16 [32], replicated
- w_b: bfloat16 [64, 32], replicated
- b_b: bfloat16 [32], replicated
- w_out: bfloat16 [1024, 128], replicated
- b_out: bfloat16 [128], replicated
Outputs:
- output: bfloat16 [256, 256, 128], P(('batch', 'dap'))
All inputs are finite; a program needn't handle non-finite values.
Results may differ from a plain program's by a relative error of at most 0.001.
Values are sent between devices in bfloat16 or wider.
A program may use at most 1 GiB of HBM per device.

v0:
```python
import jax
import jax.numpy as jnp
from jax import lax
from jax.sharding import PartitionSpec as P

LN_EPS = 1e-5
ROW_BUDGET = 8192


def layer_norm(array_b8, ln_scale, ln_offset):
    value_a7 = array_b8.astype(jnp.float32)
    mean_val = jnp.mean(value_a7, axis=-1, keepdims=True)
    centred = value_a7 - mean_val
    var_val = jnp.mean(centred * centred, axis=-1, keepdims=True)
    normed = centred * lax.rsqrt(var_val + LN_EPS)
    return (normed * ln_scale.astype(jnp.float32) + ln_offset.astype(jnp.float32)).astype(jnp.bfloat16)


def project(local_c8, weight, bias_vec):
    out_f32 = jnp.einsum('snm,mc->snc', local_c8, weight, preferred_element_type=jnp.float32)
    return (out_f32 + bias_vec.astype(jnp.float32)).astype(jnp.bfloat16)


def outer_update(z_rows, proj_a, full_b, w_out, b_out):
    n_seq, n_loc, hid_dim = proj_a.shape
    n_res = full_b.shape[1]
    pair_dim = z_rows.shape[2]
    row_tile = min(n_loc, max(1, ROW_BUDGET // n_res))
    w_cube = w_out.reshape(hid_dim, hid_dim, pair_dim)
    bias_out = b_out.astype(jnp.float32)
    inv_seq = 1.0 / n_seq

    def tile_body(tile_idx, z_acc):
        row_start = tile_idx * row_tile
        a_tile = lax.dynamic_slice_in_dim(proj_a, row_start, row_tile, axis=1)
        z_tile = lax.dynamic_slice_in_dim(z_acc, row_start, row_tile, axis=0)
        outer_prod = jnp.einsum('sic,sjd->icjd', a_tile, full_b, preferred_element_type=jnp.float32)
        outer_prod = (outer_prod * inv_seq).astype(jnp.bfloat16)
        update = jnp.einsum('icjd,cdz->ijz', outer_prod, w_cube, preferred_element_type=jnp.float32) + bias_out
        new_tile = (z_tile.astype(jnp.float32) + update).astype(jnp.bfloat16)
        return lax.dynamic_update_slice_in_dim(z_acc, new_tile, row_start, axis=0)

    return lax.fori_loop(0, n_loc // row_tile, tile_body, z_rows)


def solution(mesh):
    row_spec = P(('batch', 'dap'))
    col_spec = P(None, ('batch', 'dap'))
    rep_spec = P()

    def local_update(z_rows, value_a8, ln_scale, ln_offset, w_a, b_a, w_b, b_b, w_out, b_out):
        local_c8 = layer_norm(value_a8, ln_scale, ln_offset)
        proj_a = project(local_c8, w_a, b_a)
        proj_b = project(local_c8, w_b, b_b)
        full_b = lax.all_gather(proj_b, 'dap', axis=1, tiled=True)
        return outer_update(z_rows, proj_a, full_b, w_out, b_out)

    return jax.shard_map(local_update, mesh=mesh, in_specs=(row_spec, col_spec) + (rep_spec,) * 8, out_specs=row_spec, check_vma=False)
```

profile of v0, /device:TPU:0, one launch (start us, length us, event | category | flops | bytes accessed | tf_op | source)
XLA Modules:
  0.0 98.4 jit_solution(11185589920653846683)
XLA Ops:
  6.5 0.0 copy-start
  6.5 0.0 copy-start.1
  6.5 0.0 all-gather.2.cloned.1.call-start
  6.5 0.8 convert_element_type.41
  7.3 0.7 convert_element_type.42
  8.0 0.7 convert_element_type.46
  8.7 0.0 copy-start.3
  8.7 2.0 %convert_reduce_fusion = f32[512,32]{0,1:T(8,128)S(1)} fusion(bf16[512,32,64]{0,2,1:T(8,128)(2,1)} %param.11), kind=kLoop, calls=%fused_computation.7 | loop fusion | flops 2080768 | bytes 2162688 | tf_op jit(solution)/shard_map/reduce_sum | solution.py:12
  10.7 2.3 %fusion.10 = f32[512,32]{0,1:T(8,128)S(1)} fusion(bf16[512,32,64]{0,2,1:T(8,128)(2,1)} %param.11, f32[512,32]{0,1:T(8,128)S(1)} %broadcast_multiply_fusion), kind=kLoop, calls=%fused_computation.10 | loop fusion | flops 4177920 | bytes 2228224 | tf_op jit(solution)/shard_map/reduce_sum | solution.py:14
  13.1 0.0 copy-done.1
  13.1 0.0 copy-start.5
  13.1 0.0 copy-start.6
  13.1 0.0 copy-start.4
  13.1 0.9 fusion.13
  14.1 0.0 copy-start.2
  14.1 1.3 %copy-done.2 = bf16[512,32,64]{0,2,1:T(8,128)(2,1)} copy-done((bf16[512,32,64]{0,2,1:T(8,128)(2,1)}, bf16[512,32,64]{0,2,1:T(8,128)(2,1)S(1)}, u32[]{:S(2)}) %copy-start.2) | copy-done | bytes 2097176
  15.4 0.0 copy-done.3
  15.4 1.5 %add_convert_fusion = bf16[512,32,32]{0,2,1:T(8,128)(2,1)} fusion(bf16[512,32,64]{0,2,1:T(8,128)(2,1)S(1)} %fusion.13, f32[32]{0:T(128)S(1)} %convert_element_type.46, bf16[64,32]{0,1:T(8,128)(2,1)S(1)} %copy-done.3), kind=kOutput, calls=%fused_computation.17 | convolution fusion | flops 68157440 | bytes 3149952 | tf_op jit(solution)/shard_map/snm,mc->snc/dot_general | solution.py:20
  16.9 0.0 all-gather.2.cloned.1.call-update
  16.9 0.0 copy-done.5
  16.9 0.0 copy-done.6
  16.9 0.0 copy-done.4
  16.9 2.0 %fusion.18 = bf16[512,32,32,1]{0,2,3,1:T(8,128)(2,1)S(1)} fusion(bf16[512,32,64]{0,2,1:T(8,128)(2,1)} %copy-done.2, f32[32]{0:T(128)S(1)} %convert_element_type.44, bf16[64,32]{0,1:T(8,128)(2,1)S(1)} %copy-done.4), kind=kOutput, calls=%fused_computation.19 | convolution fusion | flops 68157440 | bytes 3149952 | tf_op jit(solution)/shard_map/snm,mc->snc/dot_general | solution.py:20
  19.0 49.2 %all-gather.2.cloned.1.call-done = bf16[512,256,32]{0,2,1:T(8,128)(2,1)} async-done(((bf16[512,32,32]{0,2,1:T(8,128)(2,1)}), bf16[512,256,32]{0,2,1:T(8,128)(2,1)}) %all-gather.2.cloned.1.call-update) | async-done | bytes 8388624 | tf_op jit(solution)/shard_map/all_gather | solution.py:55
  68.2 0.0 copy-done
  68.2 23.4 %fusion.15 = bf16[32,256,128]{2,1,0:T(8,128)(2,1)} fusion(bf16[32,256,128]{2,1,0:T(8,128)(2,1)} %param.10, bf16[512,32,32,1]{0,2,3,1:T(8,128)(2,1)S(1)} %fusion.18, bf16[512,256,32]{0,2,1:T(8,128)(2,1)} %all-gather.2.cloned.1.call-done, f32[128]{0:T(128)S(1)} %convert_element_type.49, bf16[32,32,128,1]{2,1,0,3:T(8,128)(2,1)S(1)} %bitcast.29), kind=kOutput, calls=%fused_computation.16 | convolution fusion | flops 10758389760 | bytes 13894144 | tf_op jit(solution)/shard_map/while/body/eval_jaxpr/icjd,cdz->ijz/dot_general | solution.py:39
  (4 shorter events, 0.0 us)
Async XLA Ops:
  6.5 61.7 %copy-start = (bf16[1024,128]{1,0:T(8,128)(2,1)S(1)}, bf16[1024,128]{1,0:T(8,128)(2,1)}, u32[]{:S(2)}) copy-start(bf16[1024,128]{1,0:T(8,128)(2,1)} %param.18) | copy-start | bytes 786436
  6.5 6.5 %copy-start.1 = (bf16[512,32,64]{0,2,1:T(8,128)(2,1)S(1)}, bf16[512,32,64]{0,2,1:T(8,128)(2,1)}, u32[]{:S(2)}) copy-start(bf16[512,32,64]{0,2,1:T(8,128)(2,1)} %param.11) | copy-start | bytes 6291460
  6.5 61.7 %all-gather.2.cloned.1.call-start = ((), (), s32[]{:S(2)}) async-start(), calls=%async_computation | async-start | bytes 9437184 | tf_op jit(solution)/shard_map/all_gather | solution.py:55
  8.7 6.7 %copy-start.3 = (bf16[64,32]{0,1:T(8,128)(2,1)S(1)}, bf16[64,32]{0,1:T(8,128)(2,1)}, u32[]{:S(2)}) copy-start(bf16[64,32]{0,1:T(8,128)(2,1)} %param.16) | copy-start | bytes 12292
  13.1 3.8 %copy-start.5 = (bf16[32]{0:T(256)(128)(2,1)S(1)}, bf16[32]{0:T(256)(128)(2,1)}, u32[]{:S(2)}) copy-start(bf16[32]{0:T(256)(128)(2,1)} %param.15) | copy-start | bytes 196
  13.1 3.8 %copy-start.6 = (bf16[128]{0:T(256)(128)(2,1)S(1)}, bf16[128]{0:T(256)(128)(2,1)}, u32[]{:S(2)}) copy-start(bf16[128]{0:T(256)(128)(2,1)} %param.19) | copy-start | bytes 772
  13.1 3.8 %copy-start.4 = (bf16[64,32]{0,1:T(8,128)(2,1)S(1)}, bf16[64,32]{0,1:T(8,128)(2,1)}, u32[]{:S(2)}) copy-start(bf16[64,32]{0,1:T(8,128)(2,1)} %param.14) | copy-start | bytes 12292
  14.1 1.3 %copy-start.2 = (bf16[512,32,64]{0,2,1:T(8,128)(2,1)}, bf16[512,32,64]{0,2,1:T(8,128)(2,1)S(1)}, u32[]{:S(2)}) copy-start(bf16[512,32,64]{0,2,1:T(8,128)(2,1)S(1)} %fusion.13) | copy-start | bytes 6291460
Sparse Core Ops, SparseCore 0:
  17.0 51.1 all-gather.1
where the time goes:
time: 98.6 us; the launch traced here: 98.4 us
  waiting for transfers between devices  49.2 us (50%)
  matrix products  26.9 us (27%)
  between operations  13.5 us (14%)
  other arithmetic  7.44 us (8%)
  local copies, waits for them, and re-layouts  1.34 us (1%)
    all_gather x1, waiting for transfers between devices, local_update(): full_b = lax.all_gather(proj_b, 'dap', axis=1, tiled=True)  49.2 us
    dot_general x1, matrix products, tile_body(): jnp.einsum('icjd,cdz->ijz', outer_prod, w_cube, preferred_element_type=jn...  23.4 us
    dot_general x2, matrix products, project(): jnp.einsum('snm,mc->snc', local_c8, weight, preferred_element_type=jnp.fl...  3.5 us
    reduce_sum x1, other arithmetic, layer_norm(): var_val = jnp.mean(centred * centred, axis=-1, keepdims=True)  2.32 us
    reduce_sum x1, other arithmetic, layer_norm(): mean_val = jnp.mean(value_a7, axis=-1, keepdims=True)  2.02 us
  transfers between devices with their start and end apart: 1, of which 1 were waited for; matrix products, arithmetic and copies ran while one was open for 2% of the time, Pallas kernels for 0%

commit v1 on v0

v1 whole, which is shorter than its diff:
```python
import jax
import jax.numpy as jnp
from jax import lax
from jax.experimental import pallas as pl
from jax.experimental.pallas import tpu as pltpu
from jax.sharding import PartitionSpec as P

MESH = pl.DeviceIdType.MESH
F32, BF16 = jnp.float32, jnp.bfloat16
LN_EPS = 1e-5
S, NL, M, H, N, Z = 512, 32, 64, 32, 256, 128
J = 8
NG = NL // J
CR = H * J
KR = CR // 4
NT = (((1,), (1,)), ((), ()))
NN = (((1,), (0,)), ((), ()))


def dot(x, y, dims=NN):
    return lax.dot_general(x, y, dims, preferred_element_type=F32)


def onehot(rows, cols, fn):
    r = lax.broadcasted_iota(jnp.int32, (rows, cols), 0)
    c = lax.broadcasted_iota(jnp.int32, (rows, cols), 1)
    return jnp.where(fn(r) == c, 1.0, 0.0).astype(BF16)


def kernel(z_hbm, m_hbm, lns_ref, lno_ref, wa_ref, ba_ref, wb_ref, bb_ref, wo_hbm, bo_ref, out_ref,
           b_buf, a_t, a_v, m_buf, b_f32, lhs2, w_buf, w_f32, w_v, z_buf, par,
           in_sem, send_sem, recv_sem):
    me = lax.axis_index("dap")
    core = me % 2
    xbit = (me // 2) % 2
    pt = me + 1 - 2 * core
    flip = pt - me
    xn = me + 2 - 4 * xbit
    yn = (me + 4) % 8
    dg = (xn + 4) % 8

    barrier = pltpu.get_barrier_semaphore()
    for dev in (pt, xn, yn):
        pl.semaphore_signal(barrier, inc=1, device_id={"dap": dev}, device_id_type=MESH)

    def m_copy(g):
        return pltpu.make_async_copy(m_hbm.at[pl.ds(g * J, J)], m_buf.at[g], in_sem.at[g])

    w_copy = pltpu.make_async_copy(wo_hbm, w_buf, in_sem.at[NG])
    z_copy = pltpu.make_async_copy(z_hbm, z_buf, in_sem.at[NG + 1])
    for g in range(NG):
        m_copy(g).start()
    w_copy.start()
    z_copy.start()

    def rdma(slot, g, dev, k):
        return pltpu.make_async_remote_copy(
            src_ref=b_buf.at[slot, g], dst_ref=b_buf.at[slot, g], send_sem=send_sem.at[k, g],
            recv_sem=recv_sem.at[slot, g], device_id={"dap": dev}, device_id_type=MESH)

    def arrived(slot, g):
        rdma(slot, g, pt, 0).wait_recv()

    def column(row, width):
        return jnp.broadcast_to(row.astype(F32).reshape(1, width), (128, width)).astype(BF16)

    eye = onehot(M, M, lambda r: r)
    order = onehot(2 * H, 2 * H, lambda r: jnp.where(r < H, r, H + 4 * ((r - H) % 8) + (r - H) // 8))
    w_ab = dot(order, jnp.concatenate([wa_ref[...], wb_ref[...]], axis=0)).astype(BF16)
    par[0] = dot(eye, column(lns_ref[...], M), NT)
    par[1] = dot(eye, column(lno_ref[...], M), NT)
    bias = jnp.concatenate([column(ba_ref[...], H), column(bb_ref[...], H)], axis=1)
    par[2] = dot(order, bias, NT)

    def lanes(i):
        return jnp.concatenate([par[i]] * (S // 128), axis=1)

    def produce(g, _):
        m_copy(g).wait()
        for n in range(J):
            x = m_buf[g, n].astype(F32)
            mean = jnp.sum(x, axis=0, keepdims=True) * (1.0 / M)
            x = x - mean
            var = jnp.sum(x * x, axis=0, keepdims=True) * (1.0 / M)
            x = x * lax.rsqrt(var + LN_EPS)
            x = (x * lanes(0) + lanes(1)).astype(BF16)
            r = dot(w_ab, x) + lanes(2)
            a_t[pl.ds(pl.multiple_of((g * J + n) * H, H), H), :] = r[:H].astype(BF16)
            for q in range(S // 128):
                b_f32[q, pl.ds(n, H, stride=J), :] = r[H:, 128 * q:128 * q + 128]
        b_buf[me, g] = jnp.concatenate([b_f32[q] for q in range(S // 128)], axis=1).astype(BF16)

        @pl.when(g == 0)
        def _():
            pl.semaphore_wait(barrier, 3)

        rdma(me, g, xn, 0).start()
        rdma(me, g, yn, 1).start()
        rdma(me, g, pt, 2).start()
        return 0

    lax.fori_loop(0, NG, produce, 0)

    eye256 = onehot(256, 256, lambda r: r)
    for t in range(4):
        for k in range(4):
            rows = jnp.concatenate(
                [a_t[pl.ds((8 * t + 4 * gg + (m + k) % 4) * H, H), :] for gg in range(2) for m in range(4)], axis=0)
            for h in range(S // 256):
                a_v[k, 256 * h:256 * h + 256, 256 * t:256 * t + 256] = dot(
                    eye256, rows[:, 256 * h:256 * h + 256], NT).astype(BF16)

    w_copy.wait()
    w_f32[...] = w_buf[...].astype(F32)
    for d in range(H):
        block = w_f32[pl.ds(d, H, stride=H), :].astype(BF16)
        for v in range(4):
            w_v[v, pl.ds((d // 4) * 128 + ((v - d) % 4) * H, H), :] = block
    z_copy.wait()

    bias_out = bo_ref[...].astype(F32).reshape(1, Z)
    lane = lax.broadcasted_iota(jnp.int32, (2 * KR, 128), 1) // H
    even = lane % 2 == 0
    outer = (lane == 0) | (lane == 3)
    low = lane < 2

    def unit(slot_a, g_a, slot_b, g_b):
        lhs = [jnp.concatenate([b_buf[slot_a, g_a, KR * k:KR * k + KR, :],
                                b_buf[slot_b, g_b, KR * k:KR * k + KR, :]], axis=0) for k in range(4)]
        for t in range(4):
            o = [dot(lhs[k], a_v[k, :, 256 * t:256 * t + 256]) * (1.0 / S) for k in range(4)]
            q = [[None, None] for _ in range(4)]
            for gg in range(2):
                p = [x[:, 128 * gg:128 * gg + 128] for x in o]
                e0, f0 = jnp.where(even, p[0], p[1]), jnp.where(even, p[2], p[3])
                e1, f1 = jnp.where(even, p[1], p[0]), jnp.where(even, p[3], p[2])
                q[0][gg] = jnp.where(outer, e0, f0)
                q[2][gg] = jnp.where(outer, f0, e0)
                q[1][gg] = jnp.where(low, e1, f1)
                q[3][gg] = jnp.where(low, f1, e1)
            for v in range(4):
                for c in range(2):
                    for e in range(8):
                        r0 = c * KR + e * J
                        lhs2[v, c * KR + 16 * t:c * KR + 16 * t + 16, 128 * e:128 * e + 128] = jnp.concatenate(
                            [q[v][0][r0:r0 + J], q[v][1][r0:r0 + J]], axis=0).astype(BF16)
        jc = (slot_a * NG + g_a, slot_b * NG + g_b)
        for v in range(4):
            u = dot(lhs2[v], w_v[v]) + bias_out
            for c in range(2):
                for G in range(8):
                    i = 4 * G + v
                    r0 = c * KR + G * J
                    out_ref[i, jc[c]] = (z_buf[i, jc[c]].astype(F32) + u[r0:r0 + J]).astype(BF16)

    def local(s, _):
        slot = me + flip * (s // 2)
        g = 2 * (s % 2)

        @pl.when(s >= 2)
        def _():
            arrived(slot, g)
            arrived(slot, g + 1)

        unit(slot, g, slot, g + 1)
        return 0

    lax.fori_loop(0, 4, local, 0)

    def near(s, _):
        g = s // 2
        p = s % 2
        sx, sy = xn + flip * p, yn + flip * p
        arrived(sx, g)
        arrived(sy, g)

        @pl.when(p == 0)
        def _():
            @pl.when(g % 2 == 0)
            def _():
                rdma(yn, g, xn, 3).start()

            @pl.when(g % 2 == 1)
            def _():
                rdma(xn, g, yn, 3).start()

            rdma(xn, g, pt, 4).start()
            rdma(yn, g, pt, 5).start()

        unit(sx, g, sy, g)
        return 0

    lax.fori_loop(0, 2 * NG, near, 0)

    def far(s, _):
        g = 2 * (s // 2)
        p = s % 2
        slot = dg + flip * p
        arrived(slot, g)
        arrived(slot, g + 1)

        @pl.when(p == 0)
        def _():
            rdma(dg, g, pt, 6).start()
            rdma(dg, g + 1, pt, 6).start()

        unit(slot, g, slot, g + 1)
        return 0

    lax.fori_loop(0, NG, far, 0)

    for k in range(7):
        for g in range(NG):
            rdma(me, g, pt, k).wait_send()


def local_update(z, m, lns, lno, wa, ba, wb, bb, wo, bo):
    hbm = pl.BlockSpec(memory_space=pltpu.HBM)
    vmem = pl.BlockSpec(memory_space=pltpu.VMEM)
    out = pl.pallas_call(
        kernel,
        out_shape=jax.ShapeDtypeStruct((NL, N // J, J, Z), BF16),
        in_specs=[hbm, hbm, vmem, vmem, vmem, vmem, vmem, vmem, hbm, vmem],
        out_specs=vmem,
        scratch_shapes=[
            pltpu.VMEM((8, NG, CR, S), BF16),
            pltpu.VMEM((NL * H, S), BF16),
            pltpu.VMEM((4, S, NL * H), BF16),
            pltpu.VMEM((NG, J, M, S), BF16),
            pltpu.VMEM((S // 128, CR, 128), F32),
            pltpu.VMEM((4, 2 * KR, H * H), BF16),
            pltpu.VMEM((H * H, Z), BF16),
            pltpu.VMEM((H * H, Z), F32),
            pltpu.VMEM((4, H * H, Z), BF16),
            pltpu.VMEM((NL, N // J, J, Z), BF16),
            pltpu.VMEM((3, M, 128), F32),
            pltpu.SemaphoreType.DMA((NG + 2,)),
            pltpu.SemaphoreType.DMA((7, NG)),
            pltpu.SemaphoreType.DMA((8, NG)),
        ],
        compiler_params=pltpu.CompilerParams(
            collective_id=0, has_side_effects=True, vmem_limit_bytes=48 * 1024 * 1024),
    )(z.reshape(NL, N // J, J, Z), m.transpose(1, 2, 0), lns.reshape(1, M), lno.reshape(1, M),
      wa.T, ba.reshape(1, H), wb.T, bb.reshape(1, H), wo, bo.reshape(1, Z))
    return out.reshape(NL, N, Z)


def solution(mesh):
    row, col, rep = P(("batch", "dap")), P(None, ("batch", "dap")), P()
    return jax.shard_map(local_update, mesh=mesh, in_specs=(row, col) + (rep,) * 8, out_specs=row, check_vma=False)
```

time: 98.6 us -> 51.5 us (0.52)
  waiting for transfers between devices: 49.2 us -> 0 us
  Pallas kernels: 0 us -> 42.6 us
  matrix products: 26.9 us -> 0 us
  between operations: 13.5 us -> 0.02 us
  other arithmetic: 7.44 us -> 0 us
  local copies, waits for them, and re-layouts: 1.34 us -> 8.53 us
    all_gather x1 -> x0, waiting for transfers between devices: 49.2 us -> none  [local_update(): full_b = lax.all_gather(proj_b, 'dap', axis=1, tiled=True)]
    pallas_call x0 -> x1, Pallas kernels: none -> 42.6 us  [local_update(): pl.pallas_call(kernel, out_shape=jax.ShapeDtypeStruct((NL, N // J, J, Z),...]
    dot_general x3 -> x0, matrix products: 26.9 us -> none  [the longest x1 23.4 us: tile_body(): jnp.einsum('icjd,cdz->ijz', outer_prod, w_cube, preferred_element_type=jn...]
    unnamed x14 -> x19, local copies, waits for them, and re-layouts: 1.34 us -> 8.53 us
    reduce_sum x2 -> x0, other arithmetic: 4.35 us -> none  [the longest x1 2.32 us: layer_norm(): var_val = jnp.mean(centred * centred, axis=-1, keepdims=True)]
    convert_element_type x6 -> x0, other arithmetic: 3.07 us -> none  [the longest x1 0.94 us: layer_norm(): (normed * ln_scale.astype(jnp.float32) + ln_offset.astype(jnp.float32)).a...]
  transfers between devices with their start and end apart: 1 -> 0, of which waited for: 1 -> 0; matrix products, arithmetic and copies ran while one was open for 2% -> 0% of each run, Pallas kernels for 0% -> 0%
where the time goes in v1:
time: 51.5 us; the launch traced here: 51.2 us
  Pallas kernels  42.6 us (83%)
  local copies, waits for them, and re-layouts  8.53 us (17%)
    pallas_call x1, Pallas kernels, local_update(): pl.pallas_call(kernel, out_shape=jax.ShapeDtypeStruct((NL, N // J, J, Z),...  42.6 us
    unnamed x19, local copies, waits for them, and re-layouts  8.53 us

profile of v1, /device:TPU:0, one launch (start us, length us, event | category | flops | bytes accessed | tf_op | source)
XLA Modules:
  0.0 51.2 jit_solution(5462474407413825115)
XLA Ops:
  0.0 0.0 copy-start
  0.0 1.6 %copy-done = bf16[32,256,128]{2,1,0:T(8,128)(2,1)S(1)} copy-done((bf16[32,256,128]{2,1,0:T(8,128)(2,1)S(1)}, bf16[32,256,128]{2,1,0:T(8,128)(2,1)}, u32[]{:S(2)}) %copy-start) | copy-done | bytes 2097176
  1.6 0.0 copy-start.1
  1.6 0.9 %copy-done.1 = bf16[1024,128]{1,0:T(8,128)(2,1)S(1)} copy-done((bf16[1024,128]{1,0:T(8,128)(2,1)S(1)}, bf16[1024,128]{1,0:T(8,128)(2,1)}, u32[]{:S(2)}) %copy-start.1) | copy-done | bytes 262168
  2.5 0.0 copy-start.2
  2.5 0.7 %copy-done.2 = bf16[64,32]{0,1:T(8,128)(2,1)S(1)} copy-done((bf16[64,32]{0,1:T(8,128)(2,1)S(1)}, bf16[64,32]{0,1:T(8,128)(2,1)}, u32[]{:S(2)}) %copy-start.2) | copy-done | bytes 4120
  3.2 0.0 copy-start.3
  3.2 0.7 %copy-done.3 = bf16[64,32]{0,1:T(8,128)(2,1)S(1)} copy-done((bf16[64,32]{0,1:T(8,128)(2,1)S(1)}, bf16[64,32]{0,1:T(8,128)(2,1)}, u32[]{:S(2)}) %copy-start.3) | copy-done | bytes 4120
  3.9 0.0 copy-start.4
  3.9 0.7 %copy-done.4 = bf16[64]{0:T(256)(128)(2,1)S(1)} copy-done((bf16[64]{0:T(256)(128)(2,1)S(1)}, bf16[64]{0:T(256)(128)(2,1)}, u32[]{:S(2)}) %copy-start.4) | copy-done | bytes 152
  4.6 0.0 copy-start.5
  4.6 0.7 %copy-done.5 = bf16[64]{0:T(256)(128)(2,1)S(1)} copy-done((bf16[64]{0:T(256)(128)(2,1)S(1)}, bf16[64]{0:T(256)(128)(2,1)}, u32[]{:S(2)}) %copy-start.5) | copy-done | bytes 152
  5.2 0.0 copy-start.6
  5.3 0.7 %copy-done.6 = bf16[32]{0:T(256)(128)(2,1)S(1)} copy-done((bf16[32]{0:T(256)(128)(2,1)S(1)}, bf16[32]{0:T(256)(128)(2,1)}, u32[]{:S(2)}) %copy-start.6) | copy-done | bytes 88
  5.9 0.0 copy-start.7
  5.9 0.7 %copy-done.7 = bf16[32]{0:T(256)(128)(2,1)S(1)} copy-done((bf16[32]{0:T(256)(128)(2,1)S(1)}, bf16[32]{0:T(256)(128)(2,1)}, u32[]{:S(2)}) %copy-start.7) | copy-done | bytes 88
  6.6 0.0 copy-start.8
  6.6 0.7 %copy-done.8 = bf16[128]{0:T(256)(128)(2,1)S(1)} copy-done((bf16[128]{0:T(256)(128)(2,1)S(1)}, bf16[128]{0:T(256)(128)(2,1)}, u32[]{:S(2)}) %copy-start.8) | copy-done | bytes 280
  7.2 42.6 %shard_map.100 = bf16[32,32,8,128]{3,2,1,0:T(8,128)(2,1)S(1)} custom-call(bf16[32,32,8,128]{3,2,1,0:T(8,128)(2,1)S(1)} %bitcast.11, bf16[32,64,512]{2,1,0:T(8,128)(2,1)} %bitcast.19, bf16[1,64]{1,0:T(2,128)(2,1)S(1)} %bitcast.14, bf16[1,64]{1,0:T(2,128)(2,1)S(1)} %bitcast.15, bf16[32,64]{1,0:T(8,128)(2,1)S(1)} %bitcast.12, bf16[1,32]{1,0:T(2,128)(2,1)S(1)} %bitcast.16, ...), custom_call_target="tpu_custom_call" | custom-call | tf_op jit(solution)/shard_map/pallas_call | solution.py:220
  49.9 1.3 %copy.12 = bf16[32,256,128]{2,1,0:T(8,128)(2,1)} copy(bf16[32,256,128]{2,1,0:T(8,128)(2,1)S(1)} %bitcast.10) | data formatting | bytes 4194304
Async XLA Ops:
  0.0 1.6 %copy-start = (bf16[32,256,128]{2,1,0:T(8,128)(2,1)S(1)}, bf16[32,256,128]{2,1,0:T(8,128)(2,1)}, u32[]{:S(2)}) copy-start(bf16[32,256,128]{2,1,0:T(8,128)(2,1)} %param.10) | copy-start | bytes 6291460
  1.6 0.9 %copy-start.1 = (bf16[1024,128]{1,0:T(8,128)(2,1)S(1)}, bf16[1024,128]{1,0:T(8,128)(2,1)}, u32[]{:S(2)}) copy-start(bf16[1024,128]{1,0:T(8,128)(2,1)} %wo_hbm.1) | copy-start | bytes 786436
  2.5 0.7 %copy-start.2 = (bf16[64,32]{0,1:T(8,128)(2,1)S(1)}, bf16[64,32]{0,1:T(8,128)(2,1)}, u32[]{:S(2)}) copy-start(bf16[64,32]{0,1:T(8,128)(2,1)} %param.14) | copy-start | bytes 12292
  3.2 0.7 %copy-start.3 = (bf16[64,32]{0,1:T(8,128)(2,1)S(1)}, bf16[64,32]{0,1:T(8,128)(2,1)}, u32[]{:S(2)}) copy-start(bf16[64,32]{0,1:T(8,128)(2,1)} %param.16) | copy-start | bytes 12292
  3.9 0.7 %copy-start.4 = (bf16[64]{0:T(256)(128)(2,1)S(1)}, bf16[64]{0:T(256)(128)(2,1)}, u32[]{:S(2)}) copy-start(bf16[64]{0:T(256)(128)(2,1)} %param.12) | copy-start | bytes 388
  4.6 0.7 %copy-start.5 = (bf16[64]{0:T(256)(128)(2,1)S(1)}, bf16[64]{0:T(256)(128)(2,1)}, u32[]{:S(2)}) copy-start(bf16[64]{0:T(256)(128)(2,1)} %param.13) | copy-start | bytes 388
  5.2 0.7 %copy-start.6 = (bf16[32]{0:T(256)(128)(2,1)S(1)}, bf16[32]{0:T(256)(128)(2,1)}, u32[]{:S(2)}) copy-start(bf16[32]{0:T(256)(128)(2,1)} %param.15) | copy-start | bytes 196
  5.9 0.7 %copy-start.7 = (bf16[32]{0:T(256)(128)(2,1)S(1)}, bf16[32]{0:T(256)(128)(2,1)}, u32[]{:S(2)}) copy-start(bf16[32]{0:T(256)(128)(2,1)} %param.17) | copy-start | bytes 196
  6.6 0.7 %copy-start.8 = (bf16[128]{0:T(256)(128)(2,1)S(1)}, bf16[128]{0:T(256)(128)(2,1)}, u32[]{:S(2)}) copy-start(bf16[128]{0:T(256)(128)(2,1)} %param.19) | copy-start | bytes 772

commit v2 on v1

--- a/solution.py
+++ b/solution.py
@@ -27,8 +27,9 @@
     return jnp.where(fn(r) == c, 1.0, 0.0).astype(BF16)
 
 
-def kernel(z_hbm, m_hbm, lns_ref, lno_ref, wa_ref, ba_ref, wb_ref, bb_ref, wo_hbm, bo_ref, out_ref,
+def kernel(z_hbm, m_hbm, lns_hbm, lno_hbm, wa_hbm, ba_hbm, wb_hbm, bb_hbm, wo_hbm, bo_hbm, out_ref,
            b_buf, a_t, a_v, m_buf, b_f32, lhs2, w_buf, w_f32, w_v, z_buf, par,
+           lns_ref, lno_ref, wa_ref, ba_ref, wb_ref, bb_ref, bo_ref,
            in_sem, send_sem, recv_sem):
     me = lax.axis_index("dap")
     core = me % 2
@@ -48,7 +49,13 @@
 
     w_copy = pltpu.make_async_copy(wo_hbm, w_buf, in_sem.at[NG])
     z_copy = pltpu.make_async_copy(z_hbm, z_buf, in_sem.at[NG + 1])
-    for g in range(NG):
+    small = [pltpu.make_async_copy(src, dst, in_sem.at[NG + 2 + i]) for i, (src, dst) in enumerate((
+        (lns_hbm, lns_ref), (lno_hbm, lno_ref), (wa_hbm, wa_ref), (ba_hbm, ba_ref),
+        (wb_hbm, wb_ref), (bb_hbm, bb_ref), (bo_hbm, bo_ref)))]
+    m_copy(0).start()
+    for copy in small:
+        copy.start()
+    for g in range(1, NG):
         m_copy(g).start()
     w_copy.start()
     z_copy.start()
@@ -60,6 +67,9 @@
 
     def arrived(slot, g):
         rdma(slot, g, pt, 0).wait_recv()
+
+    for copy in small:
+        copy.wait()
 
     def column(row, width):
         return jnp.broadcast_to(row.astype(F32).reshape(1, width), (128, width)).astype(BF16)
@@ -217,10 +227,12 @@
 def local_update(z, m, lns, lno, wa, ba, wb, bb, wo, bo):
     hbm = pl.BlockSpec(memory_space=pltpu.HBM)
     vmem = pl.BlockSpec(memory_space=pltpu.VMEM)
+    args = (z.reshape(NL, N // J, J, Z), m.transpose(1, 2, 0), lns.reshape(1, M), lno.reshape(1, M),
+            wa.T, ba.reshape(1, H), wb.T, bb.reshape(1, H), wo, bo.reshape(1, Z))
     out = pl.pallas_call(
         kernel,
         out_shape=jax.ShapeDtypeStruct((NL, N // J, J, Z), BF16),
-        in_specs=[hbm, hbm, vmem, vmem, vmem, vmem, vmem, vmem, hbm, vmem],
+        in_specs=[hbm] * len(args),
         out_specs=vmem,
         scratch_shapes=[
             pltpu.VMEM((8, NG, CR, S), BF16),
@@ -234,14 +246,20 @@
             pltpu.VMEM((4, H * H, Z), BF16),
             pltpu.VMEM((NL, N // J, J, Z), BF16),
             pltpu.VMEM((3, M, 128), F32),
-            pltpu.SemaphoreType.DMA((NG + 2,)),
+            pltpu.VMEM((1, M), BF16),
+            pltpu.VMEM((1, M), BF16),
+            pltpu.VMEM((H, M), BF16),
+            pltpu.VMEM((1, H), BF16),
+            pltpu.VMEM((H, M), BF16),
+            pltpu.VMEM((1, H), BF16),
+            pltpu.VMEM((1, Z), BF16),
+            pltpu.SemaphoreType.DMA((NG + 9,)),
             pltpu.SemaphoreType.DMA((7, NG)),
             pltpu.SemaphoreType.DMA((8, NG)),
         ],
         compiler_params=pltpu.CompilerParams(
             collective_id=0, has_side_effects=True, vmem_limit_bytes=48 * 1024 * 1024),
-    )(z.reshape(NL, N // J, J, Z), m.transpose(1, 2, 0), lns.reshape(1, M), lno.reshape(1, M),
-      wa.T, ba.reshape(1, H), wb.T, bb.reshape(1, H), wo, bo.reshape(1, Z))
+    )(*(pltpu.with_memory_space_constraint(x, pltpu.HBM) for x in args))
     return out.reshape(NL, N, Z)
 
 

time: 51.5 us -> 44.2 us (0.86)
  local copies, waits for them, and re-layouts: 8.53 us -> 1.32 us
    unnamed x19 -> x1, local copies, waits for them, and re-layouts: 8.53 us -> 1.32 us
where the time goes in v2:
time: 44.2 us; the launch traced here: 44.1 us
  Pallas kernels  42.8 us (97%)
  local copies, waits for them, and re-layouts  1.32 us (3%)
    pallas_call x1, Pallas kernels, local_update(): pl.pallas_call(kernel, out_shape=jax.ShapeDtypeStruct((NL, N // J, J, Z),...  42.8 us
    unnamed x1, local copies, waits for them, and re-layouts  1.32 us

profile of v2, /device:TPU:0, one launch (start us, length us, event | category | flops | bytes accessed | tf_op | source)
XLA Modules:
  0.0 44.1 jit_solution(6250134545759197859)
XLA Ops:
  0.0 42.8 %shard_map.100 = bf16[32,32,8,128]{3,2,1,0:T(8,128)(2,1)S(1)} custom-call(bf16[32,32,8,128]{3,2,1,0:T(8,128)(2,1)} %bitcast.11, bf16[32,64,512]{2,1,0:T(8,128)(2,1)} %bitcast.12, bf16[1,64]{1,0:T(2,128)(2,1)} %bitcast.15, bf16[1,64]{1,0:T(2,128)(2,1)} %bitcast.16, bf16[32,64]{1,0:T(8,128)(2,1)} %bitcast.13, bf16[1,32]{1,0:T(2,128)(2,1)} %bitcast.17, ...), custom_call_target="tpu_custom_call" | custom-call | tf_op jit(solution)/shard_map/pallas_call | solution.py:232
  42.8 1.3 %copy.12 = bf16[32,256,128]{2,1,0:T(8,128)(2,1)} copy(bf16[32,256,128]{2,1,0:T(8,128)(2,1)S(1)} %bitcast.10) | data formatting | bytes 4194304

commit v3 on v2

v3 whole, which is shorter than its diff:
```python
import jax
import jax.numpy as jnp
from jax import lax
from jax.experimental import pallas as pl
from jax.experimental.pallas import tpu as pltpu
from jax.sharding import PartitionSpec as P

MESH = pl.DeviceIdType.MESH
F32, BF16 = jnp.float32, jnp.bfloat16
LN_EPS = 1e-5
S, NL, M, H, N, Z = 512, 32, 64, 32, 256, 128
J = 8
NG = NL // J
CR = H * J
KR = CR // 4
HS = S // 2
NT = (((1,), (1,)), ((), ()))
NN = (((1,), (0,)), ((), ()))


def dot(x, y, dims=NN):
    return lax.dot_general(x, y, dims, preferred_element_type=F32)


def onehot(rows, cols, fn):
    r = lax.broadcasted_iota(jnp.int32, (rows, cols), 0)
    c = lax.broadcasted_iota(jnp.int32, (rows, cols), 1)
    return jnp.where(fn(r) == c, 1.0, 0.0).astype(BF16)


def kernel(z_hbm, m_hbm, lns_hbm, lno_hbm, wa_hbm, ba_hbm, wb_hbm, bb_hbm, wo_hbm, bo_hbm, out_ref,
           b_buf, a_t, a_v, m_buf, b_f32, lhs2, w_buf, w_f32, w_v, z_buf, par,
           lns_ref, lno_ref, wa_ref, ba_ref, wb_ref, bb_ref, bo_ref,
           part, in_sem, send_sem, recv_sem):
    me = lax.axis_index("dap")
    core = me % 2
    xbit = (me // 2) % 2
    pt = me + 1 - 2 * core
    flip = pt - me
    xn = me + 2 - 4 * xbit
    yn = (me + 4) % 8
    dg = (xn + 4) % 8

    barrier = pltpu.get_barrier_semaphore()
    for dev in (pt, xn, yn):
        pl.semaphore_signal(barrier, inc=1, device_id={"dap": dev}, device_id_type=MESH)

    def m_half(h):
        return pltpu.make_async_copy(
            m_hbm.at[pl.ds(0, J), :, pl.ds(h * HS, HS)], m_buf.at[pl.ds(0, J), :, pl.ds(h * HS, HS)], in_sem.at[h])

    m_rest = pltpu.make_async_copy(m_hbm.at[pl.ds(J, NL - J)], m_buf.at[pl.ds(J, NL - J)], in_sem.at[2])
    w_copy = pltpu.make_async_copy(wo_hbm, w_buf, in_sem.at[3])
    z_copy = pltpu.make_async_copy(z_hbm, z_buf, in_sem.at[4])
    small = [pltpu.make_async_copy(src, dst, in_sem.at[5 + i]) for i, (src, dst) in enumerate((
        (lns_hbm, lns_ref), (lno_hbm, lno_ref), (wa_hbm, wa_ref), (ba_hbm, ba_ref),
        (wb_hbm, wb_ref), (bb_hbm, bb_ref), (bo_hbm, bo_ref)))]
    m_half(0).start()
    for copy in small:
        copy.start()
    m_half(1).start()
    m_rest.start()
    w_copy.start()
    z_copy.start()

    def whole(slot, g, dev, sem):
        return pltpu.make_async_remote_copy(
            src_ref=b_buf.at[slot, g], dst_ref=b_buf.at[slot, g], send_sem=send_sem.at[0],
            recv_sem=recv_sem.at[sem], device_id={"dap": dev}, device_id_type=MESH)

    def half(slot, g, h, dev, sem, k=1):
        return pltpu.make_async_remote_copy(
            src_ref=b_buf.at[slot, g, h], dst_ref=b_buf.at[slot, g, h], send_sem=send_sem.at[k],
            recv_sem=recv_sem.at[sem], device_id={"dap": dev}, device_id_type=MESH)

    def span(ref, k, sem):
        return pltpu.make_async_remote_copy(
            src_ref=ref, dst_ref=ref, send_sem=send_sem.at[k], recv_sem=recv_sem.at[sem],
            device_id={"dap": pt}, device_id_type=MESH)

    def arrived(sem):
        span(b_buf.at[0, pl.ds(0, 2)], 0, sem).wait_recv()

    def arrived_halves(sem):
        span(b_buf.at[0, 0], 0, sem).wait_recv()

    for copy in small:
        copy.wait()

    def column(row, width):
        return jnp.broadcast_to(row.astype(F32).reshape(1, width), (128, width)).astype(BF16)

    eye = onehot(M, M, lambda r: r)
    order = onehot(2 * H, 2 * H, lambda r: jnp.where(r < H, r, H + 4 * ((r - H) % 8) + (r - H) // 8))
    w_ab = dot(order, jnp.concatenate([wa_ref[...], wb_ref[...]], axis=0)).astype(BF16)
    par[0] = dot(eye, column(lns_ref[...], M), NT)
    par[1] = dot(eye, column(lno_ref[...], M), NT)
    bias = jnp.concatenate([column(ba_ref[...], H), column(bb_ref[...], H)], axis=1)
    par[2] = dot(order, bias, NT)

    def lanes(i):
        return jnp.concatenate([par[i]] * (HS // 128), axis=1)

    def produce(g, _):
        for h in range(2):
            @pl.when(g == 0)
            def _():
                m_half(h).wait()

            if h == 0:
                @pl.when(g == 1)
                def _():
                    m_rest.wait()

            for n in range(J):
                x = m_buf[g * J + n, :, HS * h:HS * h + HS].astype(F32)
                mean = jnp.sum(x, axis=0, keepdims=True) * (1.0 / M)
                x = x - mean
                var = jnp.sum(x * x, axis=0, keepdims=True) * (1.0 / M)
                x = x * lax.rsqrt(var + LN_EPS)
                x = (x * lanes(0) + lanes(1)).astype(BF16)
                r = dot(w_ab, x) + lanes(2)
                a_t[pl.ds(pl.multiple_of((g * J + n) * H, H), H), HS * h:HS * h + HS] = r[:H].astype(BF16)
                for q in range(HS // 128):
                    b_f32[q, pl.ds(n, H, stride=J), :] = r[H:, 128 * q:128 * q + 128]
            b_buf[me, g, h] = jnp.concatenate([b_f32[q] for q in range(HS // 128)], axis=1).astype(BF16)

            @pl.when(g == 0)
            def _():
                if h == 0:
                    pl.semaphore_wait(barrier, 3)
                half(me, g, h, xn, 2, 0).start()
                half(me, g, h, yn, 2, 0).start()
                half(me, g, h, pt, 0, 0).start()

        @pl.when(g > 0)
        def _():
            whole(me, g, xn, 2 + g).start()
            whole(me, g, yn, 2 + g).start()
            whole(me, g, pt, g // 2).start()

        return 0

    lax.fori_loop(0, NG, produce, 0)

    eye256 = onehot(256, 256, lambda r: r)
    for t in range(4):
        for k in range(4):
            rows = jnp.concatenate(
                [a_t[pl.ds((8 * t + 4 * gg + (m + k) % 4) * H, H), :] for gg in range(2) for m in range(4)], axis=0)
            for h in range(S // 256):
                a_v[k, 256 * h:256 * h + 256, 256 * t:256 * t + 256] = dot(
                    eye256, rows[:, 256 * h:256 * h + 256], NT).astype(BF16)

    w_copy.wait()
    w_f32[...] = w_buf[...].astype(F32)
    for d in range(H):
        block = w_f32[pl.ds(d, H, stride=H), :].astype(BF16)
        for v in range(4):
            w_v[v, pl.ds((d // 4) * 128 + ((v - d) % 4) * H, H), :] = block
    z_copy.wait()

    bias_out = bo_ref[...].astype(F32).reshape(1, Z)
    lane = lax.broadcasted_iota(jnp.int32, (2 * KR, 128), 1) // H
    even = lane % 2 == 0
    ends = (lane == 0) | (lane == 3)
    low = lane < 2

    def pair(slot_a, g_a, slot_b, g_b, k, h):
        return jnp.concatenate([b_buf[slot_a, g_a, h, KR * k:KR * k + KR, :],
                                b_buf[slot_b, g_b, h, KR * k:KR * k + KR, :]], axis=0)

    def outer(k, h, t, chunks):
        return dot(pair(*chunks, k, h), a_v[k, HS * h:HS * h + HS, 256 * t:256 * t + 256])

    def finish(chunks, product):
        for t in range(4):
            o = [product(k, t) * (1.0 / S) for k in range(4)]
            q = [[None, None] for _ in range(4)]
            for gg in range(2):
                p = [x[:, 128 * gg:128 * gg + 128] for x in o]
                e0, f0 = jnp.where(even, p[0], p[1]), jnp.where(even, p[2], p[3])
                e1, f1 = jnp.where(even, p[1], p[0]), jnp.where(even, p[3], p[2])
                q[0][gg] = jnp.where(ends, e0, f0)
                q[2][gg] = jnp.where(ends, f0, e0)
                q[1][gg] = jnp.where(low, e1, f1)
                q[3][gg] = jnp.where(low, f1, e1)
            for v in range(4):
                for c in range(2):
                    for e in range(8):
                        r0 = c * KR + e * J
                        lhs2[v, c * KR + 16 * t:c * KR + 16 * t + 16, 128 * e:128 * e + 128] = jnp.concatenate(
                            [q[v][0][r0:r0 + J], q[v][1][r0:r0 + J]], axis=0).astype(BF16)
        slot_a, g_a, slot_b, g_b = chunks
        jc = (slot_a * NG + g_a, slot_b * NG + g_b)
        for v in range(4):
            u = dot(lhs2[v], w_v[v]) + bias_out
            for c in range(2):
                for G in range(8):
                    i = 4 * G + v
                    r0 = c * KR + G * J
                    out_ref[i, jc[c]] = (z_buf[i, jc[c]].astype(F32) + u[r0:r0 + J]).astype(BF16)

    def unit(*chunks):
        lhs = [jnp.concatenate([pair(*chunks, k, h) for h in range(2)], axis=1) for k in range(4)]
        finish(chunks, lambda k, t: dot(lhs[k], a_v[k, :, 256 * t:256 * t + 256]))

    def local(s, _):
        slot = me + flip * (s // 2)
        g = 2 * (s % 2)

        @pl.when(s >= 2)
        def _():
            arrived(s % 2)

        unit(slot, g, slot, g + 1)
        return 0

    lax.fori_loop(0, 4, local, 0)

    def near(s, _):
        g = s // 2
        p = s % 2

        @pl.when(p == 0)
        def _():
            arrived(2 + g)
            for gc in range(NG):
                @pl.when(g == gc)
                def _():
                    slot, dev = (yn, xn) if gc % 2 == 0 else (xn, yn)
                    if gc < 2:
                        whole(slot, gc, dev, 10).start()
                    else:
                        @pl.when(core == 1)
                        def _():
                            half(slot, gc, 0, dev, 12).start()
                            half(slot, gc, 1, dev, 13).start()

                        @pl.when(core == 0)
                        def _():
                            half(slot, gc, 0, dev, 14).start()

            whole(xn, g, pt, 6 + g).start()
            whole(yn, g, pt, 6 + g).start()

        @pl.when(p == 1)
        def _():
            arrived(6 + g)

            @pl.when(core == 1)
            def _():
                @pl.when(g == 2)
                def _():
                    half(yn + flip, 2, 1, xn, 15).start()

                @pl.when(g == 3)
                def _():
                    half(xn + flip, 3, 1, yn, 15).start()

        unit(xn + flip * p, g, yn + flip * p, g)
        return 0

    lax.fori_loop(0, 2 * NG, near, 0)

    d1 = dg - core + 1
    d0 = dg - core

    def hand_on(slot, h, sem):
        half(slot, 2, h, pt, sem).start()
        half(slot, 3, h, pt, sem).start()

    def first_half(slot):
        for t in range(4):
            for k in range(4):
                part[slot % 2, k, :, 256 * t:256 * t + 256] = outer(k, 0, t, (slot, 2, slot, 3))

    def second_half(slot):
        chunks = (slot, 2, slot, 3)
        finish(chunks, lambda k, t: part[slot % 2, k, :, 256 * t:256 * t + 256] + outer(k, 1, t, chunks))

    def far_from():
        arrived(10)
        whole(dg, 0, pt, 11).start()
        whole(dg, 1, pt, 11).start()

    @pl.when(core == 1)
    def _():
        def far(q, _):
            @pl.when(q == 0)
            def _():
                far_from()

            @pl.when(q == 1)
            def _():
                arrived_halves(12)
                hand_on(d1, 0, 12)
                first_half(d1)
                arrived_halves(13)
                hand_on(d1, 1, 13)
                arrived(11)

            @pl.when(q == 2)
            def _():
                arrived_halves(15)
                hand_on(d0, 1, 15)
                second_half(d1)
                arrived_halves(14)

            slot = d1 - (q + 1) // 2
            g = 2 * (q // 2)
            unit(slot, g, slot, g + 1)
            return 0

        lax.fori_loop(0, 3, far, 0)

    @pl.when(core == 0)
    def _():
        def far(q, _):
            @pl.when(q == 0)
            def _():
                far_from()

            @pl.when(q == 1)
            def _():
                arrived(11)

            unit(d0 + q, 0, d0 + q, 1)
            return 0

        lax.fori_loop(0, 2, far, 0)

        def first(q, _):
            arrived_halves(12 + 2 * q)

            @pl.when(q == 1)
            def _():
                hand_on(d0, 0, 14)

            first_half(d1 - q)
            return 0

        lax.fori_loop(0, 2, first, 0)

        def second(q, _):
            arrived_halves(13 + 2 * q)
            second_half(d1 - q)
            return 0

        lax.fori_loop(0, 2, second, 0)

    span(b_buf.at[pl.ds(0, 6)], 0, 0).wait_send()

    @pl.when(core == 1)
    def _():
        span(b_buf.at[pl.ds(0, 2), pl.ds(0, 3)], 1, 0).wait_send()

    @pl.when(core == 0)
    def _():
        span(b_buf.at[0, pl.ds(0, 2)], 1, 0).wait_send()


def local_update(z, m, lns, lno, wa, ba, wb, bb, wo, bo):
    hbm = pl.BlockSpec(memory_space=pltpu.HBM)
    vmem = pl.BlockSpec(memory_space=pltpu.VMEM)
    args = (z.reshape(NL, N // J, J, Z), m.transpose(1, 2, 0), lns.reshape(1, M), lno.reshape(1, M),
            wa.T, ba.reshape(1, H), wb.T, bb.reshape(1, H), wo, bo.reshape(1, Z))
    out = pl.pallas_call(
        kernel,
        out_shape=jax.ShapeDtypeStruct((NL, N // J, J, Z), BF16),
        in_specs=[hbm] * len(args),
        out_specs=vmem,
        scratch_shapes=[
            pltpu.VMEM((8, NG, 2, CR, HS), BF16),
            pltpu.VMEM((NL * H, S), BF16),
            pltpu.VMEM((4, S, NL * H), BF16),
            pltpu.VMEM((NL, M, S), BF16),
            pltpu.VMEM((HS // 128, CR, 128), F32),
            pltpu.VMEM((4, 2 * KR, H * H), BF16),
            pltpu.VMEM((H * H, Z), BF16),
            pltpu.VMEM((H * H, Z), F32),
            pltpu.VMEM((4, H * H, Z), BF16),
            pltpu.VMEM((NL, N // J, J, Z), BF16),
            pltpu.VMEM((3, M, 128), F32),
            pltpu.VMEM((1, M), BF16),
            pltpu.VMEM((1, M), BF16),
            pltpu.VMEM((H, M), BF16),
            pltpu.VMEM((1, H), BF16),
            pltpu.VMEM((H, M), BF16),
            pltpu.VMEM((1, H), BF16),
            pltpu.VMEM((1, Z), BF16),
            pltpu.VMEM((2, 4, 2 * KR, NL * H), F32),
            pltpu.SemaphoreType.DMA((12,)),
            pltpu.SemaphoreType.DMA((2,)),
            pltpu.SemaphoreType.DMA((16,)),
        ],
        compiler_params=pltpu.CompilerParams(
            collective_id=0, has_side_effects=True, vmem_limit_bytes=48 * 1024 * 1024),
    )(*(pltpu.with_memory_space_constraint(x, pltpu.HBM) for x in args))
    return out.reshape(NL, N, Z)


def solution(mesh):
    row, col, rep = P(("batch", "dap")), P(None, ("batch", "dap")), P()
    return jax.shard_map(local_update, mesh=mesh, in_specs=(row, col) + (rep,) * 8, out_specs=row, check_vma=False)
```

time: 44.2 us -> 42.8 us (0.968)
  Pallas kernels: 42.8 us -> 41.4 us
    pallas_call x1, Pallas kernels: 42.8 us -> 41.4 us  [local_update(): pl.pallas_call(kernel, out_shape=jax.ShapeDtypeStruct((NL, N // J, J, Z),...]
where the time goes in v3:
time: 42.8 us; the launch traced here: 42.7 us
  Pallas kernels  41.4 us (97%)
  local copies, waits for them, and re-layouts  1.32 us (3%)
    pallas_call x1, Pallas kernels, local_update(): pl.pallas_call(kernel, out_shape=jax.ShapeDtypeStruct((NL, N // J, J, Z),...  41.4 us
    unnamed x1, local copies, waits for them, and re-layouts  1.32 us

profile of v3, /device:TPU:0, one launch (start us, length us, event | category | flops | bytes accessed | tf_op | source)
XLA Modules:
  0.0 42.7 jit_solution(3856911738864151389)
XLA Ops:
  0.0 41.4 %shard_map.100 = bf16[32,32,8,128]{3,2,1,0:T(8,128)(2,1)S(1)} custom-call(bf16[32,32,8,128]{3,2,1,0:T(8,128)(2,1)} %bitcast.11, bf16[32,64,512]{2,1,0:T(8,128)(2,1)} %bitcast.12, bf16[1,64]{1,0:T(2,128)(2,1)} %bitcast.15, bf16[1,64]{1,0:T(2,128)(2,1)} %bitcast.16, bf16[32,64]{1,0:T(8,128)(2,1)} %bitcast.13, bf16[1,32]{1,0:T(2,128)(2,1)} %bitcast.17, ...), custom_call_target="tpu_custom_call" | custom-call | tf_op jit(solution)/shard_map/pallas_call | solution.py:368
  41.4 1.3 %copy.12 = bf16[32,256,128]{2,1,0:T(8,128)(2,1)} copy(bf16[32,256,128]{2,1,0:T(8,128)(2,1)S(1)} %bitcast.10) | data formatting | bytes 4194304

commit v4 on v3

--- a/solution.py
+++ b/solution.py
@@ -14,6 +14,7 @@
 CR = H * J
 KR = CR // 4
 HS = S // 2
+HQ = HS // 128
 NT = (((1,), (1,)), ((), ()))
 NN = (((1,), (0,)), ((), ()))
 
@@ -45,20 +46,21 @@
     for dev in (pt, xn, yn):
         pl.semaphore_signal(barrier, inc=1, device_id={"dap": dev}, device_id_type=MESH)
 
-    def m_half(h):
-        return pltpu.make_async_copy(
-            m_hbm.at[pl.ds(0, J), :, pl.ds(h * HS, HS)], m_buf.at[pl.ds(0, J), :, pl.ds(h * HS, HS)], in_sem.at[h])
-
-    m_rest = pltpu.make_async_copy(m_hbm.at[pl.ds(J, NL - J)], m_buf.at[pl.ds(J, NL - J)], in_sem.at[2])
-    w_copy = pltpu.make_async_copy(wo_hbm, w_buf, in_sem.at[3])
+    def m_part(i):
+        part_of = pl.ds(0, J), slice(None), pl.ds(i * 128, 128)
+        return pltpu.make_async_copy(m_hbm.at[part_of], m_buf.at[part_of], in_sem.at[i])
+
+    m_rest = pltpu.make_async_copy(m_hbm.at[pl.ds(J, NL - J)], m_buf.at[pl.ds(J, NL - J)], in_sem.at[12])
+    w_copy = pltpu.make_async_copy(wo_hbm, w_buf, in_sem.at[13])
     z_copy = pltpu.make_async_copy(z_hbm, z_buf, in_sem.at[4])
     small = [pltpu.make_async_copy(src, dst, in_sem.at[5 + i]) for i, (src, dst) in enumerate((
         (lns_hbm, lns_ref), (lno_hbm, lno_ref), (wa_hbm, wa_ref), (ba_hbm, ba_ref),
         (wb_hbm, wb_ref), (bb_hbm, bb_ref), (bo_hbm, bo_ref)))]
-    m_half(0).start()
+    m_part(0).start()
     for copy in small:
         copy.start()
-    m_half(1).start()
+    for i in range(1, S // 128):
+        m_part(i).start()
     m_rest.start()
     w_copy.start()
     z_copy.start()
@@ -98,59 +100,59 @@
     bias = jnp.concatenate([column(ba_ref[...], H), column(bb_ref[...], H)], axis=1)
     par[2] = dot(order, bias, NT)
 
-    def lanes(i):
-        return jnp.concatenate([par[i]] * (HS // 128), axis=1)
+    def make(g, h, q0, nq):
+        def lanes(i):
+            return jnp.concatenate([par[i]] * nq, axis=1)
+
+        lo = HS * h + 128 * q0
+        for n in range(J):
+            x = m_buf[g * J + n, :, lo:lo + 128 * nq].astype(F32)
+            mean = jnp.sum(x, axis=0, keepdims=True) * (1.0 / M)
+            x = x - mean
+            var = jnp.sum(x * x, axis=0, keepdims=True) * (1.0 / M)
+            x = x * lax.rsqrt(var + LN_EPS)
+            x = (x * lanes(0) + lanes(1)).astype(BF16)
+            r = dot(w_ab, x) + lanes(2)
+            for q in range(nq):
+                rq = r[:, 128 * q:128 * q + 128]
+                a_t[h, q0 + q, pl.ds((g * J + n) * H, H), :] = rq[:H].astype(BF16)
+                b_f32[q0 + q, pl.ds(n, H, stride=J), :] = rq[H:]
+        for q in range(q0, q0 + nq):
+            b_buf[me, g, h, q] = b_f32[q].astype(BF16)
+
+    for i in range(S // 128):
+        m_part(i).wait()
+        h, q = i // HQ, i % HQ
+        make(0, h, q, 1)
+        if i == 0:
+            pl.semaphore_wait(barrier, 3)
+        for dev, sem in ((xn, 2), (yn, 2), (pt, 0)):
+            piece = b_buf.at[me, 0, h, q]
+            pltpu.make_async_remote_copy(
+                src_ref=piece, dst_ref=piece, send_sem=send_sem.at[0], recv_sem=recv_sem.at[sem],
+                device_id={"dap": dev}, device_id_type=MESH).start()
+    m_rest.wait()
 
     def produce(g, _):
         for h in range(2):
-            @pl.when(g == 0)
-            def _():
-                m_half(h).wait()
-
-            if h == 0:
-                @pl.when(g == 1)
-                def _():
-                    m_rest.wait()
-
-            for n in range(J):
-                x = m_buf[g * J + n, :, HS * h:HS * h + HS].astype(F32)
-                mean = jnp.sum(x, axis=0, keepdims=True) * (1.0 / M)
-                x = x - mean
-                var = jnp.sum(x * x, axis=0, keepdims=True) * (1.0 / M)
-                x = x * lax.rsqrt(var + LN_EPS)
-                x = (x * lanes(0) + lanes(1)).astype(BF16)
-                r = dot(w_ab, x) + lanes(2)
-                a_t[pl.ds(pl.multiple_of((g * J + n) * H, H), H), HS * h:HS * h + HS] = r[:H].astype(BF16)
-                for q in range(HS // 128):
-                    b_f32[q, pl.ds(n, H, stride=J), :] = r[H:, 128 * q:128 * q + 128]
-            b_buf[me, g, h] = jnp.concatenate([b_f32[q] for q in range(HS // 128)], axis=1).astype(BF16)
-
-            @pl.when(g == 0)
-            def _():
-                if h == 0:
-                    pl.semaphore_wait(barrier, 3)
-                half(me, g, h, xn, 2, 0).start()
-                half(me, g, h, yn, 2, 0).start()
-                half(me, g, h, pt, 0, 0).start()
-
-        @pl.when(g > 0)
-        def _():
-            whole(me, g, xn, 2 + g).start()
-            whole(me, g, yn, 2 + g).start()
-            whole(me, g, pt, g // 2).start()
-
+            make(g, h, 0, HQ)
+        whole(me, g, xn, 2 + g).start()
+        whole(me, g, yn, 2 + g).start()
+        whole(me, g, pt, g // 2).start()
         return 0
 
-    lax.fori_loop(0, NG, produce, 0)
+    lax.fori_loop(1, NG, produce, 0)
 
     eye256 = onehot(256, 256, lambda r: r)
     for t in range(4):
         for k in range(4):
-            rows = jnp.concatenate(
-                [a_t[pl.ds((8 * t + 4 * gg + (m + k) % 4) * H, H), :] for gg in range(2) for m in range(4)], axis=0)
-            for h in range(S // 256):
-                a_v[k, 256 * h:256 * h + 256, 256 * t:256 * t + 256] = dot(
-                    eye256, rows[:, 256 * h:256 * h + 256], NT).astype(BF16)
+            for h in range(2):
+                rows = jnp.concatenate([jnp.concatenate(
+                    [a_t[h, q, pl.ds((8 * t + 4 * gg + (m + k) % 4) * H, H), :] for gg in range(2) for m in range(4)],
+                    axis=0) for q in range(HQ)], axis=1)
+                block = dot(eye256, rows, NT).astype(BF16)
+                for gg in range(2):
+                    a_v[k, 2 * t + gg, HS * h:HS * h + HS, :] = block[:, 128 * gg:128 * gg + 128]
 
     w_copy.wait()
     w_f32[...] = w_buf[...].astype(F32)
@@ -167,11 +169,15 @@
     low = lane < 2
 
     def pair(slot_a, g_a, slot_b, g_b, k, h):
-        return jnp.concatenate([b_buf[slot_a, g_a, h, KR * k:KR * k + KR, :],
-                                b_buf[slot_b, g_b, h, KR * k:KR * k + KR, :]], axis=0)
+        return jnp.concatenate([jnp.concatenate(
+            [b_buf[slot_a, g_a, h, q, KR * k:KR * k + KR, :], b_buf[slot_b, g_b, h, q, KR * k:KR * k + KR, :]],
+            axis=0) for q in range(HQ)], axis=1)
+
+    def a_cols(k, t, lo, n):
+        return jnp.concatenate([a_v[k, 2 * t + gg, lo:lo + n, :] for gg in range(2)], axis=1)
 
     def outer(k, h, t, chunks):
-        return dot(pair(*chunks, k, h), a_v[k, HS * h:HS * h + HS, 256 * t:256 * t + 256])
+        return dot(pair(*chunks, k, h), a_cols(k, t, HS * h, HS))
 
     def finish(chunks, product):
         for t in range(4):
@@ -189,12 +195,13 @@
                 for c in range(2):
                     for e in range(8):
                         r0 = c * KR + e * J
-                        lhs2[v, c * KR + 16 * t:c * KR + 16 * t + 16, 128 * e:128 * e + 128] = jnp.concatenate(
+                        lhs2[v, e, c * KR + 16 * t:c * KR + 16 * t + 16, :] = jnp.concatenate(
                             [q[v][0][r0:r0 + J], q[v][1][r0:r0 + J]], axis=0).astype(BF16)
         slot_a, g_a, slot_b, g_b = chunks
         jc = (slot_a * NG + g_a, slot_b * NG + g_b)
         for v in range(4):
-            u = dot(lhs2[v], w_v[v]) + bias_out
+            u = dot(jnp.concatenate([lhs2[v, e] for e in range(8)], axis=1),
+                    jnp.concatenate([w_v[v], jnp.zeros((H * H, Z), BF16)], axis=1))[:, :Z] + bias_out
             for c in range(2):
                 for G in range(8):
                     i = 4 * G + v
@@ -203,7 +210,7 @@
 
     def unit(*chunks):
         lhs = [jnp.concatenate([pair(*chunks, k, h) for h in range(2)], axis=1) for k in range(4)]
-        finish(chunks, lambda k, t: dot(lhs[k], a_v[k, :, 256 * t:256 * t + 256]))
+        finish(chunks, lambda k, t: dot(lhs[k], a_cols(k, t, 0, S)))
 
     def local(s, _):
         slot = me + flip * (s // 2)
@@ -296,15 +303,15 @@
                 arrived_halves(12)
                 hand_on(d1, 0, 12)
                 first_half(d1)
+                arrived(11)
+
+            @pl.when(q == 2)
+            def _():
                 arrived_halves(13)
                 hand_on(d1, 1, 13)
-                arrived(11)
-
-            @pl.when(q == 2)
-            def _():
+                second_half(d1)
                 arrived_halves(15)
                 hand_on(d0, 1, 15)
-                second_half(d1)
                 arrived_halves(14)
 
             slot = d1 - (q + 1) // 2
@@ -371,12 +378,12 @@
         in_specs=[hbm] * len(args),
         out_specs=vmem,
         scratch_shapes=[
-            pltpu.VMEM((8, NG, 2, CR, HS), BF16),
-            pltpu.VMEM((NL * H, S), BF16),
-            pltpu.VMEM((4, S, NL * H), BF16),
+            pltpu.VMEM((8, NG, 2, HQ, CR, 128), BF16),
+            pltpu.VMEM((2, HQ, NL * H, 128), BF16),
+            pltpu.VMEM((4, NL * H // 128, S, 128), BF16),
             pltpu.VMEM((NL, M, S), BF16),
             pltpu.VMEM((HS // 128, CR, 128), F32),
-            pltpu.VMEM((4, 2 * KR, H * H), BF16),
+            pltpu.VMEM((4, 8, 2 * KR, 128), BF16),
             pltpu.VMEM((H * H, Z), BF16),
             pltpu.VMEM((H * H, Z), F32),
             pltpu.VMEM((4, H * H, Z), BF16),
@@ -390,7 +397,7 @@
             pltpu.VMEM((1, H), BF16),
             pltpu.VMEM((1, Z), BF16),
             pltpu.VMEM((2, 4, 2 * KR, NL * H), F32),
-            pltpu.SemaphoreType.DMA((12,)),
+            pltpu.SemaphoreType.DMA((14,)),
             pltpu.SemaphoreType.DMA((2,)),
             pltpu.SemaphoreType.DMA((16,)),
         ],

time: 42.8 us -> 42.7 us (level)
  no operation moved by 1% of the time
where the time goes in v4:
time: 42.7 us; the launch traced here: 42.6 us
  Pallas kernels  41.3 us (97%)
  local copies, waits for them, and re-layouts  1.32 us (3%)
    pallas_call x1, Pallas kernels, local_update(): pl.pallas_call(kernel, out_shape=jax.ShapeDtypeStruct((NL, N // J, J, Z),...  41.3 us
    unnamed x1, local copies, waits for them, and re-layouts  1.32 us

profile of v4, /device:TPU:0, one launch (start us, length us, event | category | flops | bytes accessed | tf_op | source)
XLA Modules:
  0.0 42.6 jit_solution(1639256159063433874)
XLA Ops:
  0.0 41.3 %shard_map.100 = bf16[32,32,8,128]{3,2,1,0:T(8,128)(2,1)S(1)} custom-call(bf16[32,32,8,128]{3,2,1,0:T(8,128)(2,1)} %bitcast.11, bf16[32,64,512]{2,1,0:T(8,128)(2,1)} %bitcast.12, bf16[1,64]{1,0:T(2,128)(2,1)} %bitcast.15, bf16[1,64]{1,0:T(2,128)(2,1)} %bitcast.16, bf16[32,64]{1,0:T(8,128)(2,1)} %bitcast.13, bf16[1,32]{1,0:T(2,128)(2,1)} %bitcast.17, ...), custom_call_target="tpu_custom_call" | custom-call | tf_op jit(solution)/shard_map/pallas_call | solution.py:375
  41.3 1.3 %copy.12 = bf16[32,256,128]{2,1,0:T(8,128)(2,1)} copy(bf16[32,256,128]{2,1,0:T(8,128)(2,1)S(1)} %bitcast.10) | data formatting | bytes 4194304

commit v5 on v4

--- a/solution.py
+++ b/solution.py
@@ -29,10 +29,15 @@
     return jnp.where(fn(r) == c, 1.0, 0.0).astype(BF16)
 
 
-def kernel(z_hbm, m_hbm, lns_hbm, lno_hbm, wa_hbm, ba_hbm, wb_hbm, bb_hbm, wo_hbm, bo_hbm, out_ref,
-           b_buf, a_t, a_v, m_buf, b_f32, lhs2, w_buf, w_f32, w_v, z_buf, par,
+def project(lhs2, w_v, v):
+    return dot(jnp.concatenate([lhs2[v, e] for e in range(8)], axis=1), w_v[v])
+
+
+def kernel(z_hbm, m_hbm, lns_hbm, lno_hbm, wa_hbm, ba_hbm, wb_hbm, bb_hbm, wo_hbm, bo_hbm,
+           out_ref, lhs2, w_v, z_buf, bias_ref,
+           b_buf, a_t, a_v, m_buf, b_f32, w_buf, w_f32, par,
            lns_ref, lno_ref, wa_ref, ba_ref, wb_ref, bb_ref, bo_ref,
-           part, in_sem, send_sem, recv_sem):
+           part, recv_sem, in_sem, send_sem):
     me = lax.axis_index("dap")
     core = me % 2
     xbit = (me // 2) % 2
@@ -163,6 +168,7 @@
     z_copy.wait()
 
     bias_out = bo_ref[...].astype(F32).reshape(1, Z)
+    bias_ref[...] = jnp.broadcast_to(bias_out, (8, Z))
     lane = lax.broadcasted_iota(jnp.int32, (2 * KR, 128), 1) // H
     even = lane % 2 == 0
     ends = (lane == 0) | (lane == 3)
@@ -179,7 +185,7 @@
     def outer(k, h, t, chunks):
         return dot(pair(*chunks, k, h), a_cols(k, t, HS * h, HS))
 
-    def finish(chunks, product):
+    def regroup(product):
         for t in range(4):
             o = [product(k, t) * (1.0 / S) for k in range(4)]
             q = [[None, None] for _ in range(4)]
@@ -197,20 +203,27 @@
                         r0 = c * KR + e * J
                         lhs2[v, e, c * KR + 16 * t:c * KR + 16 * t + 16, :] = jnp.concatenate(
                             [q[v][0][r0:r0 + J], q[v][1][r0:r0 + J]], axis=0).astype(BF16)
-        slot_a, g_a, slot_b, g_b = chunks
+
+    def write(slot_a, g_a, slot_b, g_b):
         jc = (slot_a * NG + g_a, slot_b * NG + g_b)
         for v in range(4):
-            u = dot(jnp.concatenate([lhs2[v, e] for e in range(8)], axis=1),
-                    jnp.concatenate([w_v[v], jnp.zeros((H * H, Z), BF16)], axis=1))[:, :Z] + bias_out
+            u = project(lhs2, w_v, v) + bias_out
             for c in range(2):
                 for G in range(8):
                     i = 4 * G + v
                     r0 = c * KR + G * J
                     out_ref[i, jc[c]] = (z_buf[i, jc[c]].astype(F32) + u[r0:r0 + J]).astype(BF16)
 
+    def regroup_whole(*chunks):
+        lhs = [jnp.concatenate([pair(*chunks, k, h) for h in range(2)], axis=1) for k in range(4)]
+        regroup(lambda k, t: dot(lhs[k], a_cols(k, t, 0, S)))
+
+    def regroup_second(slot):
+        regroup(lambda k, t: part[slot % 2, k, :, 256 * t:256 * t + 256] + outer(k, 1, t, (slot, 2, slot, 3)))
+
     def unit(*chunks):
-        lhs = [jnp.concatenate([pair(*chunks, k, h) for h in range(2)], axis=1) for k in range(4)]
-        finish(chunks, lambda k, t: dot(lhs[k], a_cols(k, t, 0, S)))
+        regroup_whole(*chunks)
+        write(*chunks)
 
     def local(s, _):
         slot = me + flip * (s // 2)
@@ -283,8 +296,8 @@
                 part[slot % 2, k, :, 256 * t:256 * t + 256] = outer(k, 0, t, (slot, 2, slot, 3))
 
     def second_half(slot):
-        chunks = (slot, 2, slot, 3)
-        finish(chunks, lambda k, t: part[slot % 2, k, :, 256 * t:256 * t + 256] + outer(k, 1, t, chunks))
+        regroup_second(slot)
+        write(slot, 2, slot, 3)
 
     def far_from():
         arrived(10)
@@ -305,21 +318,17 @@
                 first_half(d1)
                 arrived(11)
 
-            @pl.when(q == 2)
-            def _():
-                arrived_halves(13)
-                hand_on(d1, 1, 13)
-                second_half(d1)
-                arrived_halves(15)
-                hand_on(d0, 1, 15)
-                arrived_halves(14)
-
-            slot = d1 - (q + 1) // 2
-            g = 2 * (q // 2)
-            unit(slot, g, slot, g + 1)
+            unit(d1 - q, 0, d1 - q, 1)
             return 0
 
-        lax.fori_loop(0, 3, far, 0)
+        lax.fori_loop(0, 2, far, 0)
+        arrived_halves(13)
+        hand_on(d1, 1, 13)
+        second_half(d1)
+        arrived_halves(15)
+        hand_on(d0, 1, 15)
+        arrived_halves(14)
+        regroup_whole(d0, 2, d0, 3)
 
     @pl.when(core == 0)
     def _():
@@ -349,12 +358,10 @@
 
         lax.fori_loop(0, 2, first, 0)
 
-        def second(q, _):
-            arrived_halves(13 + 2 * q)
-            second_half(d1 - q)
-            return 0
-
-        lax.fori_loop(0, 2, second, 0)
+        arrived_halves(13)
+        second_half(d1)
+        arrived_halves(15)
+        regroup_second(d0)
 
     span(b_buf.at[pl.ds(0, 6)], 0, 0).wait_send()
 
@@ -365,6 +372,32 @@
     @pl.when(core == 0)
     def _():
         span(b_buf.at[0, pl.ds(0, 2)], 1, 0).wait_send()
+
+
+def last_kernel(out_ref, lhs2, w_v, z_buf, bias_ref, out_hbm, tail, sem):
+    me = lax.axis_index("dap")
+    slot = 6 - me // 2 * 2
+    for chip in range(4):
+        @pl.when(me // 2 == chip)
+        def _():
+            hole = NG * (6 - 2 * chip) + 2
+            for lo, n in ((0, hole), (hole + 2, N // J - hole - 2)):
+                pltpu.make_async_copy(
+                    out_ref.at[:, pl.ds(lo, n)], out_hbm.at[:, pl.ds(lo, n)], sem.at[0]).start()
+
+    first = NG * slot + 2
+    for v in range(4):
+        u = project(lhs2, w_v, v) + bias_ref[:1, :]
+        for c in range(2):
+            for G in range(8):
+                i = 4 * G + v
+                r0 = c * KR + G * J
+                tail[i, c] = (z_buf[i, first + c].astype(F32) + u[r0:r0 + J]).astype(BF16)
+    rest = pltpu.make_async_copy(tail, out_hbm.at[:, pl.ds(first, 2)], sem.at[1])
+    rest.start()
+    done = out_ref.at[:, pl.ds(0, N // J - 2)]
+    pltpu.make_async_copy(done, out_hbm.at[:, pl.ds(0, N // J - 2)], sem.at[0]).wait()
+    rest.wait()
 
 
 def local_update(z, m, lns, lno, wa, ba, wb, bb, wo, bo):
@@ -372,22 +405,25 @@
     vmem = pl.BlockSpec(memory_space=pltpu.VMEM)
     args = (z.reshape(NL, N // J, J, Z), m.transpose(1, 2, 0), lns.reshape(1, M), lno.reshape(1, M),
             wa.T, ba.reshape(1, H), wb.T, bb.reshape(1, H), wo, bo.reshape(1, Z))
-    out = pl.pallas_call(
-        kernel,
-        out_shape=jax.ShapeDtypeStruct((NL, N // J, J, Z), BF16),
+    rows = jax.ShapeDtypeStruct((NL, N // J, J, Z), BF16)
+    def scoped(*refs):
+        pl.run_scoped(lambda in_sem, send_sem: kernel(*refs, in_sem, send_sem),
+                      pltpu.SemaphoreType.DMA((14,)), pltpu.SemaphoreType.DMA((2,)))
+
+    parts = pl.pallas_call(
+        scoped,
+        out_shape=(rows, jax.ShapeDtypeStruct((4, 8, 2 * KR, 128), BF16), jax.ShapeDtypeStruct((4, H * H, Z), BF16),
+                   rows, jax.ShapeDtypeStruct((8, Z), F32)),
         in_specs=[hbm] * len(args),
-        out_specs=vmem,
+        out_specs=(vmem,) * 5,
         scratch_shapes=[
             pltpu.VMEM((8, NG, 2, HQ, CR, 128), BF16),
             pltpu.VMEM((2, HQ, NL * H, 128), BF16),
             pltpu.VMEM((4, NL * H // 128, S, 128), BF16),
             pltpu.VMEM((NL, M, S), BF16),
-            pltpu.VMEM((HS // 128, CR, 128), F32),
-            pltpu.VMEM((4, 8, 2 * KR, 128), BF16),
+            pltpu.VMEM((HQ, CR, 128), F32),
             pltpu.VMEM((H * H, Z), BF16),
             pltpu.VMEM((H * H, Z), F32),
-            pltpu.VMEM((4, H * H, Z), BF16),
-            pltpu.VMEM((NL, N // J, J, Z), BF16),
             pltpu.VMEM((3, M, 128), F32),
             pltpu.VMEM((1, M), BF16),
             pltpu.VMEM((1, M), BF16),
@@ -397,13 +433,19 @@
             pltpu.VMEM((1, H), BF16),
             pltpu.VMEM((1, Z), BF16),
             pltpu.VMEM((2, 4, 2 * KR, NL * H), F32),
-            pltpu.SemaphoreType.DMA((14,)),
-            pltpu.SemaphoreType.DMA((2,)),
             pltpu.SemaphoreType.DMA((16,)),
         ],
         compiler_params=pltpu.CompilerParams(
-            collective_id=0, has_side_effects=True, vmem_limit_bytes=48 * 1024 * 1024),
+            collective_id=0, has_side_effects=True, vmem_limit_bytes=36 * 1024 * 1024),
     )(*(pltpu.with_memory_space_constraint(x, pltpu.HBM) for x in args))
+    out = pl.pallas_call(
+        last_kernel,
+        out_shape=rows,
+        in_specs=[vmem] * 5,
+        out_specs=hbm,
+        scratch_shapes=[pltpu.VMEM((NL, 2, J, Z), BF16), pltpu.SemaphoreType.DMA((2,))],
+        compiler_params=pltpu.CompilerParams(vmem_limit_bytes=4 * 1024 * 1024),
+    )(*parts)
     return out.reshape(NL, N, Z)
 
 

time: 42.7 us -> 42.2 us (0.988)
  local copies, waits for them, and re-layouts: 1.32 us -> 0 us
  Pallas kernels: 41.3 us -> 42.1 us
    unnamed x1 -> x0, local copies, waits for them, and re-layouts: 1.32 us -> none
    pallas_call x1 -> x2, Pallas kernels: 41.3 us -> 42.1 us  [the longest x1 40.7 us: local_update(): pl.pallas_call(scoped, out_shape=(rows, jax.ShapeDtypeStruct((4, 8, 2 * K...]
where the time goes in v5:
time: 42.2 us; the launch traced here: 42.1 us
  Pallas kernels  42.1 us (100%)
    pallas_call x1, Pallas kernels, local_update(): pl.pallas_call(scoped, out_shape=(rows, jax.ShapeDtypeStruct((4, 8, 2 * K...  40.7 us
    pallas_call x1, Pallas kernels, local_update(): pl.pallas_call(last_kernel, out_shape=rows, in_specs=[vmem] * 5, out_spec...  1.35 us

profile of v5, /device:TPU:0, one launch (start us, length us, event | category | flops | bytes accessed | tf_op | source)
XLA Modules:
  0.0 42.1 jit_solution(8624158660660867738)
XLA Ops:
  0.0 40.7 %shard_map.100 = (bf16[32,32,8,128]{3,2,1,0:T(8,128)(2,1)S(1)}, bf16[4,8,128,128]{3,2,1,0:T(8,128)(2,1)S(1)}, bf16[4,1024,128]{2,1,0:T(8,128)(2,1)S(1)}, bf16[32...) custom-call(bf16[32,32,8,128]{3,2,1,0:T(8,128)(2,1)} %bitcast.10, bf16[32,64,512]{2,1,0:T(8,128)(2,1)} %bitcast.11, ...), custom_call_target="tpu_custom_call" | custom-call | tf_op jit(solution)/shard_map/pallas_call | solution.py:413
  40.7 1.3 %shard_map.101 = bf16[32,32,8,128]{3,2,1,0:T(8,128)(2,1)} custom-call(bf16[32,32,8,128]{3,2,1,0:T(8,128)(2,1)S(1)} %get-tuple-element.10.out_ref, bf16[4,8,128,128]{3,2,1,0:T(8,128)(2,1)S(1)} %get-tuple-element.11.lhs2, bf16[4,1024,128]{2,1,0:T(8,128)(2,1)S(1)} %get-tuple-element.12.w_v, bf16[32,32,8,128]{3,2,1,0:T(8,128)(2,1)S(1)} %get-tuple-element.13.z_buf, ...), custom_call_target="tpu_custom_call" | custom-call | tf_op jit(solution)/shard_map/pallas_call | solution.py:441

commit v6 on v5

--- a/solution.py
+++ b/solution.py
@@ -61,14 +61,13 @@
     small = [pltpu.make_async_copy(src, dst, in_sem.at[5 + i]) for i, (src, dst) in enumerate((
         (lns_hbm, lns_ref), (lno_hbm, lno_ref), (wa_hbm, wa_ref), (ba_hbm, ba_ref),
         (wb_hbm, wb_ref), (bb_hbm, bb_ref), (bo_hbm, bo_ref)))]
-    m_part(0).start()
     for copy in small:
         copy.start()
+    for n in range(0, J, 2):
+        part_of = pl.ds(n, 2), slice(None), pl.ds(0, 128)
+        pltpu.make_async_copy(m_hbm.at[part_of], m_buf.at[part_of], in_sem.at[0]).start()
     for i in range(1, S // 128):
         m_part(i).start()
-    m_rest.start()
-    w_copy.start()
-    z_copy.start()
 
     def whole(slot, g, dev, sem):
         return pltpu.make_async_remote_copy(
@@ -127,6 +126,10 @@
 
     for i in range(S // 128):
         m_part(i).wait()
+        if i == 0:
+            m_rest.start()
+            w_copy.start()
+            z_copy.start()
         h, q = i // HQ, i % HQ
         make(0, h, q, 1)
         if i == 0:

time: 42.2 us -> 42.1 us (level)
  no operation moved by 1% of the time
where the time goes in v6:
time: 42.1 us; the launch traced here: 42 us
  Pallas kernels  42 us (100%)
    pallas_call x1, Pallas kernels, local_update(): pl.pallas_call(scoped, out_shape=(rows, jax.ShapeDtypeStruct((4, 8, 2 * K...  40.7 us
    pallas_call x1, Pallas kernels, local_update(): pl.pallas_call(last_kernel, out_shape=rows, in_specs=[vmem] * 5, out_spec...  1.35 us

profile of v6, /device:TPU:0, one launch (start us, length us, event | category | flops | bytes accessed | tf_op | source)
XLA Modules:
  0.0 42.0 jit_solution(1911247377660491549)
XLA Ops:
  0.0 40.7 %shard_map.100 = (bf16[32,32,8,128]{3,2,1,0:T(8,128)(2,1)S(1)}, bf16[4,8,128,128]{3,2,1,0:T(8,128)(2,1)S(1)}, bf16[4,1024,128]{2,1,0:T(8,128)(2,1)S(1)}, bf16[32...) custom-call(bf16[32,32,8,128]{3,2,1,0:T(8,128)(2,1)} %bitcast.10, bf16[32,64,512]{2,1,0:T(8,128)(2,1)} %bitcast.11, ...), custom_call_target="tpu_custom_call" | custom-call | tf_op jit(solution)/shard_map/pallas_call | solution.py:416
  40.7 1.3 %shard_map.101 = bf16[32,32,8,128]{3,2,1,0:T(8,128)(2,1)} custom-call(bf16[32,32,8,128]{3,2,1,0:T(8,128)(2,1)S(1)} %get-tuple-element.10.out_ref, bf16[4,8,128,128]{3,2,1,0:T(8,128)(2,1)S(1)} %get-tuple-element.11.lhs2, bf16[4,1024,128]{2,1,0:T(8,128)(2,1)S(1)} %get-tuple-element.12.w_v, bf16[32,32,8,128]{3,2,1,0:T(8,128)(2,1)S(1)} %get-tuple-element.13.z_buf, ...), custom_call_target="tpu_custom_call" | custom-call | tf_op jit(solution)/shard_map/pallas_call | solution.py:444
